TPU v7x, 8 devices: a whole 2x2x1 slice. The times are simulated.
8 devices in a mesh: data: 2 (over z, y), seq: 4 (over x, core).
Axes of the slice: x: 2, y: 2, z: 1, core: 2. Of those that a mesh axis runs over, the one named last changes fastest.
Arguments:
- dec_in: bfloat16 [2048, 768], P(('data', 'seq')), parts along dimension 0
- memory: bfloat16 [16384, 768], P(('data', 'seq')), parts along dimension 0
- mem_len: int32 [2], P('data'), parts along dimension 0
- grad_out: float32 [2048, 768], P(('data', 'seq')), parts along dimension 0
- norm_attn: bfloat16 [768], replicated
- wq_cross: bfloat16 [768, 12, 64], replicated
- wk_cross: bfloat16 [768, 12, 64], replicated
- wv_cross: bfloat16 [768, 12, 64], replicated
- wo_cross: bfloat16 [12, 64, 768], replicated
- norm_mlp: bfloat16 [768], replicated
- w_gate: bfloat16 [768, 3072], replicated
- w_up: bfloat16 [768, 3072], replicated
- w_down: bfloat16 [3072, 768], replicated
Outputs:
- output 1: float32 [2048, 768], P(('data', 'seq')), parts along dimension 0
- output 2: float32 [16384, 768], P(('data', 'seq')), parts along dimension 0
- output 3: float32 [1536], P('data'), parts along dimension 0
- output 4: float32 [1536, 12, 64], P('data'), parts along dimension 0
- output 5: float32 [1536, 12, 64], P('data'), parts along dimension 0
- output 6: float32 [1536, 12, 64], P('data'), parts along dimension 0
- output 7: float32 [24, 64, 768], P('data'), parts along dimension 0
- output 8: float32 [1536], P('data'), parts along dimension 0
- output 9: float32 [1536, 3072], P('data'), parts along dimension 0
- output 10: float32 [1536, 3072], P('data'), parts along dimension 0
- output 11: float32 [6144, 768], P('data'), parts along dimension 0
There are 2 independent parts. A program takes and returns all parts, laid end to end along the dimension named above; an argument that names none is the same for every part.
All inputs are finite; a program needn't handle non-finite values.
Results may differ from a plain program's by a relative error of at most 0.013332.
Values are sent between devices in bfloat16 or wider.
A program may use at most 1 GiB of HBM per device.

v0:
```python
import jax
import jax.numpy as jnp
from jax import lax
from jax.sharding import PartitionSpec as P


def rms_norm(tensor, gain):
    mean_sq = jnp.mean(tensor * tensor, axis=-1, keepdims=True)
    return tensor * lax.rsqrt(mean_sq + 1e-6) * gain


def gated_unit(gate_pre, up_pre):
    return jax.nn.silu(gate_pre) * up_pre


def solution(mesh):
    group_size = mesh.shape['seq']
    row_spec = P(('data', 'seq'), None)
    weight_spec = P()
    part_vec = P('data')
    part_mat = P('data', None)
    part_cube = P('data', None, None)

    def device_step(dec_in, memory, mem_len, grad_out, norm_attn, wq_cross, wk_cross, wv_cross, wo_cross, norm_mlp, w_gate, w_up, w_down):
        q_rows, model_dim = dec_in.shape
        m_rows = memory.shape[0]
        heads, head_dim = wq_cross.shape[1], wq_cross.shape[2]
        kv_heads = wk_cross.shape[1]
        head_group = heads // kv_heads
        score_scale = head_dim ** -0.5
        wo_grouped = wo_cross.reshape(kv_heads, head_group, head_dim, model_dim)
        mem_pos = lax.axis_index('seq') * m_rows + jnp.arange(m_rows)
        valid_mask = mem_pos < mem_len[0]

        x_in = dec_in.astype(jnp.float32)
        normed_f, norm_pull = jax.vjp(rms_norm, x_in, norm_attn.astype(jnp.float32))
        normed = normed_f.astype(jnp.bfloat16)
        local_query = jnp.einsum('td,dhe->the', normed, wq_cross, preferred_element_type=jnp.float32).astype(jnp.bfloat16)
        dec_query = lax.all_gather(local_query, 'seq', axis=0, tiled=True).reshape(q_rows * group_size, kv_heads, head_group, head_dim)
        mem_keys = jnp.einsum('td,dke->tke', memory, wk_cross, preferred_element_type=jnp.float32).astype(jnp.bfloat16)
        mem_vals = jnp.einsum('td,dke->tke', memory, wv_cross, preferred_element_type=jnp.float32).astype(jnp.bfloat16)

        def masked_scores():
            raw_scores = jnp.einsum('qkge,tke->kqgt', dec_query, mem_keys, preferred_element_type=jnp.float32)
            return jnp.where(valid_mask, raw_scores * score_scale, -1e30)

        scores = masked_scores()
        local_max = jnp.max(scores, axis=-1)
        exp_scores = jnp.exp(scores - local_max[..., None])
        local_sum = jnp.sum(exp_scores, axis=-1)
        local_out = jnp.einsum('kqgt,tke->kqge', exp_scores.astype(jnp.bfloat16), mem_vals, preferred_element_type=jnp.float32)
        global_max = lax.pmax(local_max, 'seq')
        rescale = jnp.exp(local_max - global_max)
        out_sum = lax.psum_scatter(local_out * rescale[..., None], 'seq', scatter_dimension=1, tiled=True)
        den_sum = lax.psum_scatter(local_sum * rescale, 'seq', scatter_dimension=1, tiled=True)
        attended_f = out_sum / den_sum[..., None]
        attended = attended_f.astype(jnp.bfloat16)
        hidden_f = x_in + jnp.einsum('kqge,kged->qd', attended, wo_grouped, preferred_element_type=jnp.float32)
        hidden = hidden_f.astype(jnp.bfloat16)
        normed_mlp_f, mlp_norm_pull = jax.vjp(rms_norm, hidden.astype(jnp.float32), norm_mlp.astype(jnp.float32))
        normed_mlp = normed_mlp_f.astype(jnp.bfloat16)
        gate_pre = jnp.dot(normed_mlp, w_gate, preferred_element_type=jnp.float32)
        up_pre = jnp.dot(normed_mlp, w_up, preferred_element_type=jnp.float32)
        mlp_f, gated_pull = jax.vjp(gated_unit, gate_pre, up_pre)
        mlp_act = mlp_f.astype(jnp.bfloat16)

        grad_top = grad_out.astype(jnp.bfloat16)
        g_down = jnp.einsum('qf,qd->fd', mlp_act, grad_top, preferred_element_type=jnp.float32)
        grad_act = jnp.einsum('qd,fd->qf', grad_top, w_down, preferred_element_type=jnp.float32)
        grad_gate, grad_up = gated_pull(grad_act)
        grad_gate_b = grad_gate.astype(jnp.bfloat16)
        grad_up_b = grad_up.astype(jnp.bfloat16)
        g_gate = jnp.einsum('qd,qf->df', normed_mlp, grad_gate_b, preferred_element_type=jnp.float32)
        g_up = jnp.einsum('qd,qf->df', normed_mlp, grad_up_b, preferred_element_type=jnp.float32)
        grad_normed_mlp = (jnp.einsum('qf,df->qd', grad_gate_b, w_gate, preferred_element_type=jnp.float32)
                           + jnp.einsum('qf,df->qd', grad_up_b, w_up, preferred_element_type=jnp.float32))
        grad_hidden_norm, g_norm_mlp = mlp_norm_pull(grad_normed_mlp)
        grad_hidden = grad_out + grad_hidden_norm
        grad_hidden_b = grad_hidden.astype(jnp.bfloat16)
        g_wo = jnp.einsum('kqge,qd->kged', attended, grad_hidden_b, preferred_element_type=jnp.float32).reshape(heads, head_dim, model_dim)
        grad_attended = jnp.einsum('qd,kged->kqge', grad_hidden_b, wo_grouped, preferred_element_type=jnp.float32)
        row_delta = jnp.sum(grad_attended * attended_f, axis=-1)
        grad_att_all = lax.all_gather(grad_attended.astype(jnp.bfloat16), 'seq', axis=1, tiled=True)
        stats = lax.all_gather(jnp.stack([den_sum, row_delta]), 'seq', axis=2, tiled=True)
        attn_prob = jnp.exp(masked_scores() - global_max[..., None]) / stats[0][..., None]
        grad_prob = jnp.einsum('kqge,tke->kqgt', grad_att_all, mem_vals, preferred_element_type=jnp.float32)
        grad_scores = (attn_prob * (grad_prob - stats[1][..., None]) * score_scale).astype(jnp.bfloat16)
        grad_vals = jnp.einsum('kqgt,kqge->tke', attn_prob.astype(jnp.bfloat16), grad_att_all, preferred_element_type=jnp.float32)
        grad_keys = jnp.einsum('kqgt,qkge->tke', grad_scores, dec_query, preferred_element_type=jnp.float32)
        grad_query_part = jnp.einsum('kqgt,tke->kqge', grad_scores, mem_keys, preferred_element_type=jnp.float32)
        grad_query = lax.psum_scatter(grad_query_part, 'seq', scatter_dimension=1, tiled=True)
        grad_query_b = jnp.transpose(grad_query, (1, 0, 2, 3)).reshape(q_rows, heads, head_dim).astype(jnp.bfloat16)
        g_wq = jnp.einsum('td,the->dhe', normed, grad_query_b, preferred_element_type=jnp.float32)
        grad_normed = jnp.einsum('the,dhe->td', grad_query_b, wq_cross, preferred_element_type=jnp.float32)
        grad_x_norm, g_norm_attn = norm_pull(grad_normed)
        g_dec = grad_hidden + grad_x_norm
        grad_keys_b = grad_keys.astype(jnp.bfloat16)
        grad_vals_b = grad_vals.astype(jnp.bfloat16)
        g_wk = jnp.einsum('td,tke->dke', memory, grad_keys_b, preferred_element_type=jnp.float32)
        g_wv = jnp.einsum('td,tke->dke', memory, grad_vals_b, preferred_element_type=jnp.float32)
        g_mem = (jnp.einsum('tke,dke->td', grad_keys_b, wk_cross, preferred_element_type=jnp.float32)
                 + jnp.einsum('tke,dke->td', grad_vals_b, wv_cross, preferred_element_type=jnp.float32))
        weight_grads = lax.psum((g_norm_attn, g_wq, g_wk, g_wv, g_wo, g_norm_mlp, g_gate, g_up, g_down), 'seq')
        return (g_dec, g_mem) + tuple(weight_grads)

    return jax.shard_map(device_step, mesh=mesh,
                         in_specs=(row_spec, row_spec, part_vec, row_spec) + (weight_spec,) * 9,
                         out_specs=(row_spec, row_spec, part_vec, part_cube, part_cube, part_cube, part_cube, part_vec, part_mat, part_mat, part_mat),
                         check_vma=False)
```

profile of v0, /device:TPU:0, one launch (start us, length us, event | category | flops | bytes accessed | tf_op | source)
XLA Modules:
  0.0 1043.9 jit_solution(12006867059956379980)
XLA Ops:
  7.2 0.8 convert_element_type.86
  8.1 1.2 fusion.57
  9.3 0.5 copy-done.30
  9.9 2.0 fusion.74
  11.9 0.8 convert_element_type.88
  12.7 0.0 reduce-scatter.6.cloned.1.call-start
  13.4 5.9 fusion.95
  19.3 4.5 fusion.96
  23.8 8.7 all-gather.3.cloned.1.call-done
  32.5 37.7 %fusion.2 = (f32[12,1024]{1,0:T(8,128)S(1)}, f32[12,1024,2048]{2,1,0:T(8,128)}) fusion(pred[2048]{0:T(1024)(128)(4,1)S(1)} %add_compare_fusion, bf16[1024,12,64]{0,2,1:T(8,128)(2,1)} %all-gather.3.cloned.1.call-done, f32[2048,12,64]{0,2,1:T(8,128)} %bitcast.126), kind=kOutput, calls=%fused_computation.6 | convolution fusion | flops 3298283520 | bytes 108578816 | tf_op jit(solution)/shard_map/qkge,tke->kqgt/dot_general | solution.py:44
  70.1 31.3 %fusion = f32[12,1024]{1,0:T(8,128)S(1)} fusion(f32[12,1024,2048]{2,1,0:T(8,128)} %get-tuple-element.33, f32[12,1024]{1,0:T(8,128)S(1)} %get-tuple-element.32, pred[2048]{0:T(1024)(128)(4,1)S(1)} %add_compare_fusion), kind=kLoop, calls=%fused_computation.4 | loop fusion | flops 100651008 | bytes 100763648 | tf_op jit(solution)/shard_map/reduce_sum | solution.py:50
  101.4 10.9 %pmax.7 = f32[12,1024,1]{1,0,2:T(8,128)S(1)} all-reduce(f32[12,1024,1]{1,0,2:T(8,128)S(1)} %bitcast.134), channel_id=1, replica_groups=mesh['data'=2,'seq'=4] {'seq'}, use_global_device_ids=true, to_apply=%region_2.3 | all-reduce | flops 12288 | bytes 98304 | tf_op jit(solution)/shard_map/pmax | solution.py:52
  112.3 0.7 bitcast_multiply_fusion
  112.9 0.0 reduce-scatter.4.cloned.1.call-start
  113.0 36.8 %multiply_bitcast_fusion = f32[12,1024,1,64]{1,3,0,2:T(8,128)} fusion(f32[12,1024,2048]{2,1,0:T(8,128)} %get-tuple-element.33, f32[12,1024]{1,0:T(8,128)S(1)} %get-tuple-element.32, pred[2048]{0:T(1024)(128)(4,1)S(1)} %add_compare_fusion, f32[12,1024]{1,0:T(8,128)S(1)} %get-tuple-element.31, f32[2048,12,64]{0,2,1:T(8,128)} %bitcast.150), kind=kOutput, calls=%fused_computation.31 | convolution fusion | flops 3324248064 | bytes 110200832 | tf_op jit(solution)/shard_map/kqgt,tke->kqge/dot_general | solution.py:51
  149.9 0.2 all-gather.5.cloned.1.call-start
  150.1 0.4 copy-done.33
  150.5 32.5 %reduce-scatter.4.cloned.1.call-done = f32[12,256,1,64]{1,3,0,2:T(8,128)} async-done(((f32[12,1024,1,64]{1,3,0,2:T(8,128)}), f32[12,256,1,64]{1,3,0,2:T(8,128)}) %reduce-scatter.4.cloned.1.call-update) | async-done | bytes 786448 | tf_op jit(solution)/shard_map/reduce_scatter | solution.py:54
  183.0 2.3 fusion.55
  185.3 4.0 fusion.90
  189.4 1.5 fusion.92
  190.9 0.1 copy-done.37
  191.0 0.1 copy-done.18
  191.1 0.5 slice-done.4
  191.6 2.6 multiply_convert_fusion.2
  194.3 1.5 fusion.97
  195.9 0.0 copy-done.11
  195.9 2.4 fusion.52
  198.3 0.2 fusion.53
  198.6 0.9 copy-done.1
  199.4 1.9 fusion.94
  201.4 0.9 pad_maximum_fusion
  202.3 8.4 all_gather.10
  210.7 0.7 slice_bitcast_fusion.1
  211.3 3.3 fusion.61
  214.6 5.3 fusion.88
  219.9 5.3 fusion.86
  225.2 5.8 fusion.36
  231.0 61.4 %multiply_convert_fusion = bf16[12,1024,2048]{2,1,0:T(8,128)(2,1)} fusion(f32[12,1024]{1,0:T(8,128)S(1)} %copy-done.27, f32[12,1024]{1,0:T(8,128)S(1)} %copy-done.26, f32[12,1024]{1,0:T(8,128)S(1)} %bitcast.135, f32[12,1024,2048]{2,1,0:T(8,128)} %get-tuple-element.33, pred[2048]{0:T(1024)(128)(4,1)S(1)} %add_compare_fusion, ...), kind=kOutput, calls=%fused_computation | convolution fusion | flops 3424124928 | bytes 159008768 | tf_op jit(solution)/shard_map/kqge,tke->kqgt/dot_general | solution.py:86
  292.4 23.7 %convolution_bitcast_fusion = f32[12,1024,1,64]{1,3,0,2:T(8,128)} fusion(bf16[12,1024,2048]{2,1,0:T(8,128)(2,1)} %multiply_convert_fusion, f32[2048,12,64]{0,2,1:T(8,128)} %bitcast.127), kind=kOutput, calls=%fused_computation.32 | convolution fusion | flops 3222798336 | bytes 59768832 | tf_op jit(solution)/shard_map/kqgt,tke->kqge/dot_general | solution.py:90
  316.2 0.2 all-reduce.4.cloned.1.call-start
  316.4 35.8 %fusion.8 = bf16[12,64,2048]{2,1,0:T(8,128)(2,1)S(1)} fusion(f32[12,1024]{1,0:T(8,128)S(1)} %copy-done.26, f32[12,1024]{1,0:T(8,128)S(1)} %bitcast.136, f32[12,1024,2048]{2,1,0:T(8,128)} %get-tuple-element.33, pred[2048]{0:T(1024)(128)(4,1)S(1)} %add_compare_fusion, bf16[12,1024,1,64]{1,3,0,2:T(8,128)(2,1)} %all-gather.5.cloned.1.call-done), kind=kOutput, calls=%fused_computation.13 | convolution fusion | flops 3348627456 | bytes 105482240 | tf_op jit(solution)/shard_map/kqgt,kqge->tke/dot_general | solution.py:88
  352.3 19.3 %convolution_convert_fusion = bf16[12,64,2048]{2,1,0:T(8,128)(2,1)S(1)} fusion(bf16[1024,12,64]{0,2,1:T(8,128)(2,1)S(1)} %copy-done.4, bf16[12,1024,2048]{2,1,0:T(8,128)(2,1)} %multiply_convert_fusion), kind=kOutput, calls=%fused_computation.14 | convolution fusion | flops 3222798336 | bytes 55050240 | tf_op jit(solution)/shard_map/kqgt,qkge->tke/dot_general | solution.py:89
  371.6 4.0 fusion.26
  375.6 4.0 fusion.31
  379.6 1.2 convert_element_type.102
  380.8 0.8 copy-done.15
  381.6 2.0 fusion.72
  383.6 5.0 fusion.21
  388.7 4.6 bitcast_add_fusion
  393.3 2.1 fusion.50
  395.4 7.2 all-reduce
  402.6 0.7 multiply_multiply_fusion
  403.2 2.5 fusion.54
  405.7 600.1 %all-reduce.4.cloned.1.call-done = (f32[768,12,64]{0,2,1:T(8,128)}, f32[768,12,64]{0,2,1:T(8,128)}, f32[768,12,64]{0,2,1:T(8,128)}, f32[12,64,768]{2,1,0:T(8,128...) async-done(((f32[768,12,64]{0,2,1:T(8,128)}, f32[768,12,64]{0,2,1:T(8,128)}, f32[768,12,64]{0,2,1:T(8,128)}, f32[12,64,768]{2,1,0:T(8,128)}, ...) | async-done | bytes 37748752 | tf_op jit(solution)/shard_map/psum | solution.py:103
  1005.8 3.4 copy.32
  1009.2 1.4 copy.33
  1010.6 1.1 copy-done.9
  1011.7 1.4 copy.34
  1013.1 1.1 copy-done.8
  1014.2 1.4 copy.35
  1015.6 8.8 copy.36
  1024.4 8.7 copy.37
  1033.1 3.7 copy.38
  (114 shorter events, 0.5 us)
Async XLA Ops:
  7.2 6.2 copy-start
  7.2 25.3 %all-gather.3.cloned.1.call-start = ((), (), s32[]{:S(2)}) async-start(), calls=%async_computation.3 | async-start | bytes 1966080 | tf_op jit(solution)/shard_map/all_gather | solution.py:39
  8.1 1.8 copy-start.23
  9.3 0.6 copy-start.30
  9.9 2.0 copy-start.28
  12.7 137.9 %reduce-scatter.6.cloned.1.call-start = ((), (), s32[]{:S(2)}) async-start(), calls=%async_computation.5 | async-start | bytes 81920 | tf_op jit(solution)/shard_map/reduce_scatter | solution.py:55
  13.4 5.9 copy-start.35
  112.3 0.7 copy-start.21
  112.9 70.1 %reduce-scatter.4.cloned.1.call-start = ((), (), s32[]{:S(2)}) async-start(), calls=%async_computation.4 | async-start | bytes 3932160 | tf_op jit(solution)/shard_map/reduce_scatter | solution.py:54
  149.9 0.7 copy-start.33
  149.9 33.1 %copy-start.2 = (bf16[256,768]{1,0:T(8,128)(2,1)S(1)}, bf16[256,768]{1,0:T(8,128)(2,1)}, u32[]{:S(2)}) copy-start(bf16[256,768]{1,0:T(8,128)(2,1)} %param.13) | copy-start | bytes 1179652
  149.9 81.1 %all-gather.5.cloned.1.call-start = ((), (), s32[]{:S(2)}) async-start(), calls=%async_computation.6 | async-start | bytes 1966080 | tf_op jit(solution)/shard_map/all_gather | solution.py:83
  183.0 6.3 slice-start.7
  185.3 13.0 %copy-start.5 = (bf16[256,768]{1,0:T(8,128)(2,1)}, bf16[256,768]{1,0:T(8,128)(2,1)S(1)}, u32[]{:S(2)}) copy-start(bf16[256,768]{1,0:T(8,128)(2,1)S(1)} %get-tuple-element.35) | copy-start | bytes 1179652
  185.3 4.0 slice-start.8
  185.3 5.6 slice-start.3
  189.3 1.6 copy-start.37
  189.4 1.7 copy-start.18
  189.4 2.2 slice-start.4
  189.4 4.9 slice-start.5
  191.6 2.6 copy-start.39
  191.6 2.7 slice-start.6
  194.2 1.6 copy-start.13
  194.3 1.7 copy-start.11
  195.9 3.5 copy-start.20
  195.9 3.5 copy-start.25
  195.9 3.5 copy-start.34
  198.6 0.9 copy-start.1
  201.3 13.3 %copy-start.6 = (bf16[256,768]{1,0:T(8,128)(2,1)S(1)}, bf16[256,768]{1,0:T(8,128)(2,1)}, u32[]{:S(2)}) copy-start(bf16[256,768]{1,0:T(8,128)(2,1)} %copy-done.5) | copy-start | bytes 1179652
  201.4 178.3 %reduce-scatter.8.cloned.1.call-start = ((), (), s32[]{:S(2)}) async-start(), calls=%async_computation.7 | async-start | bytes 3932160 | tf_op jit(solution)/shard_map/reduce_scatter | solution.py:91
  201.4 13.2 %copy-start.14 = (bf16[256,3072]{1,0:T(8,128)(2,1)S(1)}, bf16[256,3072]{1,0:T(8,128)(2,1)}, u32[]{:S(2)}) copy-start(bf16[256,3072]{1,0:T(8,128)(2,1)} %copy-done.13) | copy-start | bytes 4718596
  214.6 5.3 copy-start.12
  219.9 5.3 copy-start.19
  219.9 5.3 copy-start.38
  219.9 5.3 copy-start.40
  225.2 5.9 copy-start.22
  225.2 5.9 copy-start.26
  225.2 5.9 copy-start.27
  316.2 689.7 %all-reduce.4.cloned.1.call-start = ((), (), s32[]{:S(2)}) async-start(), calls=%async_computation.8 | async-start | bytes 75497472 | tf_op jit(solution)/shard_map/psum | solution.py:103
  316.4 35.9 %copy-start.4 = (bf16[1024,12,64]{0,2,1:T(8,128)(2,1)S(1)}, bf16[1024,12,64]{0,2,1:T(8,128)(2,1)}, u32[]{:S(2)}) copy-start(bf16[1024,12,64]{0,2,1:T(8,128)(2,1)} %all-gather.3.cloned.1.call-done) | copy-start | bytes 4718596
  352.3 23.3 %copy-start.41 = (bf16[12,64,2048]{2,1,0:T(8,128)(2,1)}, bf16[12,64,2048]{2,1,0:T(8,128)(2,1)S(1)}, u32[]{:S(2)}) copy-start(bf16[12,64,2048]{2,1,0:T(8,128)(2,1)S(1)} %fusion.8) | copy-start | bytes 9437188
  371.5 4.0 copy-start.7
  375.6 6.0 copy-start.3
  375.6 6.0 copy-start.24
  375.6 6.0 copy-start.29
  380.8 0.8 copy-start.15
  383.6 5.1 copy-start.36
  383.6 5.1 copy-start.42
  388.7 4.6 copy-start.16
  388.7 4.6 copy-start.17
  393.3 2.1 copy-start.32
  393.3 9.3 copy-start.31
  1005.8 3.4 copy-start.10
  1009.2 2.5 copy-start.9
  1011.7 2.5 copy-start.8
  1015.6 17.4 %slice-start = ((s8[9437184]{0:T(1024)(128)(4,1)}), s8[4194304]{0:T(1024)(128)(4,1)S(1)}, s32[]{:S(2)}) async-start(s8[9437184]{0:T(1024)(128)(4,1)} %bitcast.129), calls=%async_computation.9 | async-start | bytes 8388608
  1015.6 17.4 %slice-start.1 = ((s8[9437184]{0:T(1024)(128)(4,1)}), s8[4194304]{0:T(1024)(128)(4,1)S(1)}, s32[]{:S(2)}) async-start(s8[9437184]{0:T(1024)(128)(4,1)} %bitcast.129), calls=%async_computation.10 | async-start | bytes 8388608
  1024.4 8.7 slice-start.2
Sparse Core Ops, SparseCore 0:
  12.8 19.6 all-gather.2
  113.1 15.1 reduce-scatter.5
  150.0 32.9 reduce-scatter.3
  201.5 17.3 all-gather.4
  316.3 33.0 reduce-scatter.7
  383.7 622.0 all-reduce.3
where the time goes:
time: 1050 us; the launch traced here: 1040 us
  waiting for transfers between devices  641 us (61%)
  matrix products  285 us (27%)
  other arithmetic  40.2 us (4%)
  local copies, waits for them, and re-layouts  35.2 us (3%)
  blocking collectives  26.4 us (3%)
  between operations  15.5 us (1%)
    psum x1, waiting for transfers between devices, device_step(): lax.psum((g_norm_attn, g_wq, g_wk, g_wv, g_wo, g_norm_mlp, g_gate, g_up,...  600 us
    dot_general x1, matrix products, device_step(): jnp.einsum('kqge,tke->kqgt', grad_att_all, mem_vals, preferred_element_ty...  61.4 us
    dot_general x1, matrix products, masked_scores(): jnp.einsum('qkge,tke->kqgt', dec_query, mem_keys, preferred_element_type=...  37.7 us
    dot_general x1, matrix products, device_step(): jnp.einsum('kqgt,tke->kqge', exp_scores.astype(jnp.bfloat16), mem_vals, p...  36.8 us
    dot_general x1, matrix products, device_step(): jnp.einsum('kqgt,kqge->tke', attn_prob.astype(jnp.bfloat16), grad_att_all...  35.8 us
    unnamed x111, local copies, waits for them, and re-layouts  34.6 us
    reduce_scatter x1, waiting for transfers between devices, device_step(): lax.psum_scatter(local_out * rescale[..., None], 'seq', scatter_dimension...  32.5 us
    reduce_sum x1, other arithmetic, device_step(): local_sum = jnp.sum(exp_scores, axis=-1)  31.3 us
  transfers between devices with their start and end apart: 6, of which 3 were waited for; matrix products, arithmetic and copies ran while one was open for 14% of the time, Pallas kernels for 0%

commit v1 on v0

v1 whole, which is shorter than its diff:
```python
import functools

import jax
import jax.numpy as jnp
from jax import lax
from jax.experimental import pallas as pl
from jax.experimental.pallas import tpu as pltpu
from jax.sharding import PartitionSpec as P

LOG2E = 1.4426950408889634
NEG = -1e30
BF = jnp.bfloat16
F32 = jnp.float32
FKB = 512
FQB = 512
BKB = 256
BQB = 512
PAIR = 128
OROWS = 72


def dot(a, b):
    return jnp.dot(a, b, preferred_element_type=F32)


def fwd_kernel(len_ref, qt_ref, k0_ref, k1_ref, vt0_ref, vt1_ref, o_ref, m_ref, l_ref, acc_ref, qz_ref):
    qb = qt_ref.shape[1]
    half = lax.broadcasted_iota(jnp.int32, (PAIR, qb), 0) // 64
    for h in range(2):
        qz_ref[h] = jnp.where(half == h, qt_ref[...], jnp.zeros((), BF))
    m_ref[...] = jnp.full(m_ref.shape, NEG, F32)
    l_ref[...] = jnp.zeros(l_ref.shape, F32)
    acc_ref[...] = jnp.zeros(acc_ref.shape, F32)

    for seg, (k_ref, vt_ref) in enumerate(((k0_ref, vt0_ref), (k1_ref, vt1_ref))):
        count = len_ref[seg]

        def step(j, masked):
            rows = pl.ds(pl.multiple_of(j * FKB, FKB), FKB)
            kb = k_ref[rows, :]
            for h in range(2):
                st = dot(kb, qz_ref[h])
                if masked:
                    pos = lax.broadcasted_iota(jnp.int32, st.shape, 0) + j * FKB
                    st = jnp.where(pos < count, st, NEG)
                m_old = m_ref[h]
                m_new = jnp.maximum(m_old, jnp.max(st, axis=0, keepdims=True))
                p = jnp.exp2((st - m_new) * LOG2E)
                alpha = jnp.exp2((m_old - m_new) * LOG2E)
                l_ref[h] = l_ref[h] * alpha + jnp.sum(p, axis=0, keepdims=True)
                pv = dot(vt_ref[h * 64:(h + 1) * 64, rows], p.astype(BF))
                acc_ref[h] = acc_ref[h] * alpha + pv
                m_ref[h] = m_new

        full = count // FKB

        @pl.loop(0, full)
        def _(j):
            step(j, False)

        @pl.when(full * FKB < count)
        def _():
            step(full, True)

    for h in range(2):
        o_ref[h, 0:64, :] = acc_ref[h]
        o_ref[h, 64:72, :] = jnp.concatenate(
            [m_ref[h], l_ref[h], jnp.zeros((6, qb), F32)], axis=0)


def attention_forward(lens, qt, k0, k1, vt0, vt1, pair0, pairs):
    nq = qt.shape[1]
    rows = k0.shape[0]
    off = pair0
    spec = pltpu.PrefetchScalarGridSpec(
        num_scalar_prefetch=1,
        grid=(pairs, nq // FQB),
        in_specs=[
            pl.BlockSpec((PAIR, FQB), lambda p, i, s: (p + off, i)),
            pl.BlockSpec((rows, PAIR), lambda p, i, s: (0, p + off)),
            pl.BlockSpec((rows, PAIR), lambda p, i, s: (0, p + off)),
            pl.BlockSpec((PAIR, rows), lambda p, i, s: (p + off, 0)),
            pl.BlockSpec((PAIR, rows), lambda p, i, s: (p + off, 0)),
        ],
        out_specs=pl.BlockSpec((2, OROWS, FQB), lambda p, i, s: (p, 0, i)),
        scratch_shapes=[
            pltpu.VMEM((2, 1, FQB), F32),
            pltpu.VMEM((2, 1, FQB), F32),
            pltpu.VMEM((2, 64, FQB), F32),
            pltpu.VMEM((2, PAIR, FQB), BF),
        ])
    work = 2 * pairs * nq * 2 * rows
    return pl.pallas_call(
        fwd_kernel,
        out_shape=jax.ShapeDtypeStruct((2 * pairs, OROWS, nq), F32),
        grid_spec=spec,
        compiler_params=pltpu.CompilerParams(vmem_limit_bytes=48 << 20),
        cost_estimate=pl.CostEstimate(flops=work * 256 * 2, bytes_accessed=8 << 20, transcendentals=work),
        name="attn_fwd",
    )(lens, qt, k0, k1, vt0, vt1)


def bwd_kernel(len_ref, qt_ref, q_ref, dot_ref, do_ref, lse_ref, dl_ref,
               k0_ref, k1_ref, v0_ref, v1_ref, kt0_ref, kt1_ref,
               dk0_ref, dk1_ref, dv0_ref, dv1_ref, dqt_ref,
               qzt_ref, qz_ref, dozt_ref, doz_ref):
    nq = q_ref.shape[0]
    half_r = lax.broadcasted_iota(jnp.int32, (PAIR, nq), 0) // 64
    half_c = lax.broadcasted_iota(jnp.int32, (nq, PAIR), 1) // 64
    zero = jnp.zeros((), BF)
    for h in range(2):
        qzt_ref[h] = jnp.where(half_r == h, qt_ref[...], zero)
        dozt_ref[h] = jnp.where(half_r == h, dot_ref[...], zero)
        qz_ref[h] = jnp.where(half_c == h, q_ref[...], zero)
        doz_ref[h] = jnp.where(half_c == h, do_ref[...], zero)
    dqt_ref[...] = jnp.zeros(dqt_ref.shape, F32)

    segs = ((k0_ref, v0_ref, kt0_ref, dk0_ref, dv0_ref), (k1_ref, v1_ref, kt1_ref, dk1_ref, dv1_ref))
    for seg, (k_ref, v_ref, kt_ref, dk_ref, dv_ref) in enumerate(segs):
        count = len_ref[seg]
        blocks = k_ref.shape[0] // BKB

        def step(j, masked):
            rows = pl.ds(pl.multiple_of(j * BKB, BKB), BKB)
            kb, vb = k_ref[rows, :], v_ref[rows, :]
            dk = jnp.zeros((BKB, PAIR), F32)
            dv = jnp.zeros((BKB, PAIR), F32)
            for h in range(2):
                ktb = kt_ref[h * 64:(h + 1) * 64, rows]
                for c in range(nq // BQB):
                    cols = slice(c * BQB, (c + 1) * BQB)
                    st = dot(kb, qzt_ref[h, :, cols])
                    p = jnp.exp2((st - lse_ref[h, :, cols]) * LOG2E)
                    if masked:
                        pos = lax.broadcasted_iota(jnp.int32, st.shape, 0) + j * BKB
                        p = jnp.where(pos < count, p, 0.0)
                    dp = dot(vb, dozt_ref[h, :, cols])
                    ds = (p * (dp - dl_ref[h, :, cols])).astype(BF)
                    dv = dv + dot(p.astype(BF), doz_ref[h, cols, :])
                    dk = dk + dot(ds, qz_ref[h, cols, :])
                    dqt_ref[h, :, cols] += dot(ktb, ds)
            dk_ref[rows, :] = dk.astype(BF)
            dv_ref[rows, :] = dv.astype(BF)

        full = count // BKB

        @pl.loop(0, full)
        def _(j):
            step(j, False)

        @pl.when(full * BKB < count)
        def _():
            step(full, True)

        @pl.loop((count + BKB - 1) // BKB, blocks)
        def _(j):
            rows = pl.ds(pl.multiple_of(j * BKB, BKB), BKB)
            dk_ref[rows, :] = jnp.zeros((BKB, PAIR), BF)
            dv_ref[rows, :] = jnp.zeros((BKB, PAIR), BF)


def attention_backward(lens, qt, q, dot_t, do, lse, delta, k0, k1, v0, v1, kt0, kt1, pair0, pairs):
    nq = q.shape[0]
    rows = k0.shape[0]
    off = pair0
    across = pl.BlockSpec((PAIR, nq), lambda p, s: (p + off, 0))
    down = pl.BlockSpec((nq, PAIR), lambda p, s: (0, p + off))
    stat = pl.BlockSpec((2, 1, nq), lambda p, s: (p + off, 0, 0))
    keys = pl.BlockSpec((rows, PAIR), lambda p, s: (0, p + off))
    keys_t = pl.BlockSpec((PAIR, rows), lambda p, s: (p + off, 0))
    keys_out = pl.BlockSpec((rows, PAIR), lambda p, s: (0, p))
    spec = pltpu.PrefetchScalarGridSpec(
        num_scalar_prefetch=1,
        grid=(pairs,),
        in_specs=[across, down, across, down, stat, stat, keys, keys, keys, keys, keys_t, keys_t],
        out_specs=[keys_out] * 4 + [pl.BlockSpec((2, 64, nq), lambda p, s: (p, 0, 0))],
        scratch_shapes=[
            pltpu.VMEM((2, PAIR, nq), BF), pltpu.VMEM((2, nq, PAIR), BF),
            pltpu.VMEM((2, PAIR, nq), BF), pltpu.VMEM((2, nq, PAIR), BF),
        ])
    work = 2 * pairs * nq * 2 * rows
    key_out = jax.ShapeDtypeStruct((rows, pairs * PAIR), BF)
    return pl.pallas_call(
        bwd_kernel,
        out_shape=[key_out] * 4 + [jax.ShapeDtypeStruct((2 * pairs, 64, nq), F32)],
        grid_spec=spec,
        compiler_params=pltpu.CompilerParams(vmem_limit_bytes=56 << 20),
        cost_estimate=pl.CostEstimate(flops=work * 640 * 2, bytes_accessed=16 << 20, transcendentals=work),
        name="attn_bwd",
    )(lens, qt, q, dot_t, do, lse, delta, k0, k1, v0, v1, kt0, kt1)


def inv_rms(tensor):
    return lax.rsqrt(jnp.mean(tensor * tensor, axis=-1, keepdims=True) + 1e-6)


def norm_back(unit, inv, gain, grad):
    scaled = grad * gain
    return inv * (scaled - unit * jnp.mean(scaled * unit, axis=-1, keepdims=True))


def mm(a, b, ca, cb, dtype=F32):
    out = lax.dot_general(a, b, (((ca,), (cb,)), ((), ())), preferred_element_type=F32)
    return out if dtype == F32 else out.astype(dtype)


def solution(mesh):
    n = mesh.shape['seq']
    near = [(i, i ^ 1) for i in range(n)]
    far = [(i, i ^ 2) for i in range(n)]
    row_spec = P(('data', 'seq'), None)
    weight_spec = P()
    part_vec = P('data')
    part_mat = P('data', None)
    part_cube = P('data', None, None)

    def to_near(a):
        return lax.ppermute(a, 'seq', near)

    def to_far(a):
        return lax.ppermute(a, 'seq', far)

    def device_step(dec_in, memory, mem_len, grad_out, norm_attn, wq, wk, wv, wo, norm_mlp, w_gate, w_up, w_down):
        rows, dim = dec_in.shape
        m_rows = memory.shape[0]
        heads, head = wq.shape[1], wq.shape[2]
        mine = heads // 2
        width = mine * head
        dev = lax.axis_index('seq')
        core = lax.rem(dev, 2)
        wq2, wk2, wv2 = (w.reshape(dim, heads * head) for w in (wq, wk, wv))
        wo2 = wo.reshape(heads * head, dim)
        lens = jnp.stack([jnp.clip(mem_len[0] - i * m_rows, 0, m_rows) for i in (dev, dev ^ 1)]).astype(jnp.int32)

        def gather_rows(a):
            across = to_far(a)
            out = jnp.zeros((n * rows,) + a.shape[1:], a.dtype)
            for part, who in ((a, dev), (across, dev ^ 2), (to_near(a), dev ^ 1), (to_near(across), dev ^ 3)):
                out = lax.dynamic_update_slice(out, part, (who * rows, 0))
            return out

        def my_cols(w):
            return lax.dynamic_slice(w, (0, core * width), (dim, width))

        x_all_b = gather_rows(dec_in)
        mem_near = to_near(memory)
        g_all = gather_rows(grad_out)
        gain1 = norm_attn.astype(F32)
        gain2 = norm_mlp.astype(F32)

        wq_m, wk_m, wv_m = my_cols(wq2), my_cols(wk2), my_cols(wv2)
        kv = []
        for mem in (memory, mem_near):
            kv.append((mm(mem, wk_m, 1, 0, BF), mm(mem, wv_m, 1, 0, BF),
                       mm(wk_m, mem, 0, 1, BF), mm(wv_m, mem, 0, 1, BF)))
        (k0, v0, kt0, vt0), (k1, v1, kt1, vt1) = kv

        x_all = x_all_b.astype(F32)
        inv1 = inv_rms(x_all)
        unit1 = x_all * inv1
        n1 = (unit1 * gain1).astype(BF)
        q = mm(n1, wq_m, 1, 0, BF)
        scale = jnp.asarray(head ** -0.5, BF)
        q_s = q * scale
        qt_s = q_s.T

        groups = [(0, 1), (1, 1), (2, 1)]
        parts = []
        for pair0, pairs in groups:
            part = attention_forward(lens, qt_s, k0, k1, vt0, vt1, pair0, pairs)
            parts.append((part, to_far(part)))
        outs, lses = [], []
        for a, b in parts:
            ma, mb = a[:, 64:65], b[:, 64:65]
            top = jnp.maximum(ma, mb)
            ea, eb = jnp.exp(ma - top), jnp.exp(mb - top)
            den = a[:, 65:66] * ea + b[:, 65:66] * eb
            outs.append((a[:, :64] * ea + b[:, :64] * eb) / den)
            lses.append(top + jnp.log(den))
        o_t = jnp.concatenate(outs, axis=0)
        lse = jnp.concatenate(lses, axis=0)
        o_t_b = o_t.astype(BF).reshape(width, n * rows)
        o_t_near = to_near(o_t_b)

        wo_m = lax.dynamic_slice(wo2, (core * width, 0), (width, dim))
        wo_n = lax.dynamic_slice(wo2, ((1 - core) * width, 0), (width, dim))
        hidden = (x_all + mm(o_t_b, wo_m, 0, 0) + mm(o_t_near, wo_n, 0, 0)).astype(BF)

        hid = hidden.astype(F32)
        inv2 = inv_rms(hid)
        unit2 = hid * inv2
        n2 = (unit2 * gain2).astype(BF)
        g_top = g_all.astype(BF)
        grad_act = mm(g_top, w_down, 1, 1)
        gate = mm(n2, w_gate, 1, 0)
        up = mm(n2, w_up, 1, 0)
        sig = jax.nn.sigmoid(gate)
        act = gate * sig
        mlp_act = (act * up).astype(BF)
        d_up = (grad_act * act).astype(BF)
        d_gate = (grad_act * up * (sig * (1.0 + gate * (1.0 - sig)))).astype(BF)
        d_n2 = mm(d_gate, w_gate, 1, 1) + mm(d_up, w_up, 1, 1)
        g_norm_mlp = jnp.sum(d_n2 * unit2, axis=0)
        d_hid = g_all + norm_back(unit2, inv2, gain2, d_n2)
        d_hid_b = d_hid.astype(BF)

        do_t_f = mm(wo_m, d_hid_b, 1, 1)
        delta = jnp.sum(do_t_f.reshape(mine, head, n * rows) * o_t, axis=1, keepdims=True)
        do_t = do_t_f.astype(BF)
        do = mm(d_hid_b, wo_m, 1, 1, BF)
        dks, dvs, dqs, dws = [], [], [], []
        for pair0, pairs in groups:
            dk0, dk1, dv0, dv1, dqt = attention_backward(
                lens, qt_s, q_s, do_t, do, lse, delta, k0, k1, v0, v1, kt0, kt1, pair0, pairs)
            dqs.append(dqt + to_far(dqt))
            dkv0 = jnp.concatenate([dk0, dv0], axis=1)
            dkv1 = jnp.concatenate([dk1, dv1], axis=1)
            dw = mm(memory, dkv0, 0, 0) + mm(mem_near, dkv1, 0, 0)
            dws.append(dw + to_far(dw))
            dks.append((dkv0, to_near(dkv1)))
        wide = PAIR
        dwk_m = jnp.concatenate([w[:, :wide] for w in dws], axis=1)
        dwv_m = jnp.concatenate([w[:, wide:] for w in dws], axis=1)
        dw_m = jnp.stack([dwk_m, dwv_m])
        dw_n = to_near(dw_m)
        low = jnp.where(core == 0, dw_m, dw_n)
        high = jnp.where(core == 0, dw_n, dw_m)
        dw_all = jnp.concatenate([low, high], axis=2).reshape(2, dim, heads, head)
        g_wk, g_wv = dw_all[0], dw_all[1]

        mine_kv = jnp.concatenate([a for a, _ in dks], axis=1)
        near_kv = jnp.concatenate([b for _, b in dks], axis=1)

        def pair_rows(wk_x, wv_x):
            cols = []
            for i in range(width // wide):
                cols += [wk_x[:, i * wide:(i + 1) * wide], wv_x[:, i * wide:(i + 1) * wide]]
            return jnp.concatenate(cols, axis=1)

        def near_cols(w):
            return lax.dynamic_slice(w, (0, (1 - core) * width), (dim, width))

        g_mem = (mm(mine_kv, pair_rows(wk_m, wv_m), 1, 1)
                 + mm(near_kv, pair_rows(near_cols(wk2), near_cols(wv2)), 1, 1))

        dqt_b = (jnp.concatenate(dqs, axis=0) * (head ** -0.5)).astype(BF).reshape(width, n * rows)
        dqt_near = to_near(dqt_b)
        dwq_m = mm(n1, dqt_b, 0, 1)
        dwq_n = mm(n1, dqt_near, 0, 1)
        g_wq = jnp.concatenate([jnp.where(core == 0, dwq_m, dwq_n), jnp.where(core == 0, dwq_n, dwq_m)],
                               axis=1).reshape(dim, heads, head)
        d_n1 = mm(dqt_b, wq_m, 0, 1) + mm(dqt_near, near_cols(wq2), 0, 1)
        g_norm_attn = jnp.sum(d_n1 * unit1, axis=0)
        d_x = d_hid + norm_back(unit1, inv1, gain1, d_n1)
        g_dec = lax.dynamic_slice(d_x, (dev * rows, 0), (rows, dim))

        gwo_m = mm(o_t_b, d_hid_b, 1, 0)
        gwo_n = mm(o_t_near, d_hid_b, 1, 0)
        g_wo = jnp.concatenate([jnp.where(core == 0, gwo_m, gwo_n), jnp.where(core == 0, gwo_n, gwo_m)],
                               axis=0).reshape(heads, head, dim)
        g_gate = mm(n2, d_gate, 0, 0)
        g_up = mm(n2, d_up, 0, 0)
        g_down = mm(mlp_act, g_top, 0, 0)
        return (g_dec, g_mem, g_norm_attn, g_wq, g_wk, g_wv, g_wo, g_norm_mlp, g_gate, g_up, g_down)

    return jax.shard_map(device_step, mesh=mesh,
                         in_specs=(row_spec, row_spec, part_vec, row_spec) + (weight_spec,) * 9,
                         out_specs=(row_spec, row_spec, part_vec, part_cube, part_cube, part_cube, part_cube,
                                    part_vec, part_mat, part_mat, part_mat),
                         check_vma=False)
```

time: 1050 us -> 453 us (0.43)
  the two profiles are of different devices: /device:TPU:0 before, /device:TPU:5 now
where the time goes in v1:
time: 453 us; the launch traced here: 449 us
  matrix products  152 us (34%)
  Pallas kernels  145 us (32%)
  waiting for transfers between devices  64.5 us (14%)
  local copies, waits for them, and re-layouts  47.2 us (10%)
  other arithmetic  20.2 us (4%)
  starting transfers between devices  18.3 us (4%)
    dot_general x31, matrix products, mm(): lax.dot_general(a, b, (((ca,), (cb,)), ((), ())), preferred_element_type=...  152 us
    pallas_call x3, Pallas kernels, attention_backward(): pl.pallas_call(bwd_kernel, out_shape=[key_out] * 4 + [jax.ShapeDtypeStruc...  84.1 us
    ppermute x11, waiting for transfers between devices, to_far(): return lax.ppermute(a, 'seq', far)  64.5 us
    pallas_call x3, Pallas kernels, attention_forward(): pl.pallas_call(fwd_kernel, out_shape=jax.ShapeDtypeStruct((2 * pairs, ORO...  60.4 us
    unnamed x122, local copies, waits for them, and re-layouts  15.5 us
    dynamic_update_slice x8, local copies, waits for them, and re-layouts, gather_rows(): out = lax.dynamic_update_slice(out, part, (who * rows, 0))  13.3 us
    ppermute x11, starting transfers between devices, to_near(): return lax.ppermute(a, 'seq', near)  12.3 us
    convert_element_type x4, local copies, waits for them, and re-layouts, mm(): return out if dtype == F32 else out.astype(dtype)  10.7 us
  transfers between devices with their start and end apart: 22, of which 5 were waited for; matrix products, arithmetic and copies ran while one was open for 24% of the time, Pallas kernels for 13%

profile of v1, /device:TPU:5, one launch (start us, length us, event | category | flops | bytes accessed | tf_op | source)
XLA Modules:
  0.0 449.0 jit_solution(5998866214891099020)
XLA Ops:
  3.9 2.3 copy.24
  7.1 2.0 dynamic-slice_dynamic-update-slice_fusion.5
  14.3 2.6 convolution_convert_fusion.3.kt0_ref
  16.8 3.0 convolution_convert_fusion.1
  21.7 2.4 copy.33.k0_ref
  24.1 3.1 copy.35.vt0_ref
  27.3 2.1 broadcast_in_dim.6
  29.3 2.1 constant_dynamic-update-slice_fusion.19
  31.4 1.8 constant_dynamic-update-slice_fusion.14
  33.9 1.8 constant_dynamic-update-slice_fusion.12
  35.7 1.8 fusion.13
  38.2 3.6 fusion.24.q_ref
  43.4 4.7 %convolution_convert_fusion.2.kt1_ref = bf16[384,2048]{1,0:T(8,128)(2,1)} fusion(bf16[2048,768]{1,0:T(8,128)(2,1)} %collective-permute-done.6, bf16[768,768]{0,1:T(8,128)(2,1)} %bitcast.120, s32[]{:T(128)S(6)} %select_n.69), kind=kOutput, calls=%fused_computation.38 | convolution fusion | flops 1208745984 | bytes 5308420 | tf_op jit(solution)/shard_map/dot_general | solution.py:203
  48.0 2.6 copy.34.k1_ref
  50.6 5.1 %convolution_convert_fusion = bf16[384,2048]{0,1:T(8,128)(2,1)} fusion(bf16[2048,768]{1,0:T(8,128)(2,1)} %collective-permute-done.6, bf16[768,768]{0,1:T(8,128)(2,1)} %bitcast.124, s32[]{:T(128)S(6)} %select_n.69), kind=kOutput, calls=%fused_computation.36 | convolution fusion | flops 1208745984 | bytes 5308420 | tf_op jit(solution)/shard_map/dot_general | solution.py:203
  55.7 2.6 copy.36.vt1_ref
  61.1 20.1 %attn_fwd.3 = f32[2,72,1024]{2,1,0:T(8,128)S(1)} custom-call(s32[2]{0:T(128)S(1)} %pad_add_fusion.len_ref, bf16[384,1024]{1,0:T(8,128)(2,1)S(1)} %copy.32.qt_ref, bf16[2048,384]{1,0:T(8,128)(2,1)S(1)} %copy.33.k0_ref, bf16[2048,384]{1,0:T(8,128)(2,1)S(1)} %copy-done.2, bf16[384,2048]{1,0:T(8,128)(2,1)S(1)} %copy-done.3, bf16[384,2048]{1,0:T(8,128)(2,1)} %copy.36.vt1_ref), custom_call_target="tpu_custom_call" | custom-call | flops 4294967296 | bytes 8388608 | tf_op jit(solution)/shard_map/attn_fwd/pallas_call | solution.py:93
  81.2 20.2 %attn_fwd.4 = f32[2,72,1024]{2,1,0:T(8,128)S(1)} custom-call(s32[2]{0:T(128)S(1)} %pad_add_fusion.len_ref, bf16[384,1024]{1,0:T(8,128)(2,1)S(1)} %copy.32.qt_ref, bf16[2048,384]{1,0:T(8,128)(2,1)S(1)} %copy.33.k0_ref, bf16[2048,384]{1,0:T(8,128)(2,1)S(1)} %copy-done.2, bf16[384,2048]{1,0:T(8,128)(2,1)S(1)} %copy-done.3, bf16[384,2048]{1,0:T(8,128)(2,1)} %copy.36.vt1_ref), custom_call_target="tpu_custom_call" | custom-call | flops 4294967296 | bytes 8388608 | tf_op jit(solution)/shard_map/attn_fwd/pallas_call | solution.py:93
  101.5 20.1 %attn_fwd.5 = f32[2,72,1024]{2,1,0:T(8,128)S(1)} custom-call(s32[2]{0:T(128)S(1)} %pad_add_fusion.len_ref, bf16[384,1024]{1,0:T(8,128)(2,1)S(1)} %copy.32.qt_ref, bf16[2048,384]{1,0:T(8,128)(2,1)S(1)} %copy.33.k0_ref, bf16[2048,384]{1,0:T(8,128)(2,1)S(1)} %copy-done.2, bf16[384,2048]{1,0:T(8,128)(2,1)S(1)} %copy-done.3, bf16[384,2048]{1,0:T(8,128)(2,1)} %copy.36.vt1_ref), custom_call_target="tpu_custom_call" | custom-call | flops 4294967296 | bytes 8388608 | tf_op jit(solution)/shard_map/attn_fwd/pallas_call | solution.py:93
  122.0 14.1 %collective-permute-done.9 = f32[2,72,1024]{2,1,0:T(8,128)S(1)} collective-permute-done((f32[2,72,1024]{2,1,0:T(8,128)S(1)}, f32[2,72,1024]{2,1,0:T(8,128)S(1)}, u32[]{:S(2)}, u32[]{:S(2)}) %collective-permute-start.9) | collective-permute-done | bytes 589856 | tf_op jit(solution)/shard_map/ppermute | solution.py:221
  137.7 2.1 constant_dynamic-update-slice_fusion.18
  139.8 2.1 constant_dynamic-update-slice_fusion.17
  141.8 2.1 constant_dynamic-update-slice_fusion.16
  145.6 3.1 fusion.12
  148.8 8.5 %fusion.93 = f32[1024,3072]{1,0:T(8,128)} fusion(bf16[768,3072]{1,0:T(8,128)(2,1)S(1)} %bitcast.100, bf16[1024,768]{0,1:T(8,128)(2,1)S(1)} %get-tuple-element.101, f32[768]{0:T(1024)S(1)} %convert_element_type.100, f32[1024]{0:T(1024)S(1)} %add_rsqrt_fusion), kind=kOutput, calls=%fused_computation.204 | convolution fusion | flops 4834983936 | bytes 18881536 | tf_op jit(solution)/shard_map/dot_general | solution.py:203
  157.4 8.3 %fusion.95 = f32[1024,3072]{1,0:T(8,128)} fusion(bf16[768,3072]{1,0:T(8,128)(2,1)S(1)} %bitcast.102, bf16[1024,768]{0,1:T(8,128)(2,1)S(1)} %get-tuple-element.101, f32[768]{0:T(1024)S(1)} %convert_element_type.100, f32[1024]{0:T(1024)S(1)} %add_rsqrt_fusion), kind=kOutput, calls=%fused_computation.205 | convolution fusion | flops 4834983936 | bytes 18881536 | tf_op jit(solution)/shard_map/dot_general | solution.py:203
  165.6 15.9 %fusion.1 = f32[3072,768]{1,0:T(8,128)} fusion(f32[1024,3072]{1,0:T(8,128)} %fusion.95, f32[1024,3072]{1,0:T(8,128)} %fusion.93, f32[1024,768]{0,1:T(8,128)} %constant_dynamic-update-slice_fusion.16), kind=kOutput, calls=%fused_computation.5 | convolution fusion | flops 4851499008 | bytes 37748736 | tf_op jit(solution)/shard_map/dot_general | solution.py:203
  181.5 20.8 %multiply_convert_fusion.1 = (bf16[1024,3072]{1,0:T(8,128)(2,1)}, bf16[1024,3072]{1,0:T(8,128)(2,1)}) fusion(f32[1024,3072]{1,0:T(8,128)} %fusion.93, f32[1024,3072]{1,0:T(8,128)} %fusion.95, bf16[3072,768]{1,0:T(8,128)(2,1)} %param.25, f32[1024,768]{0,1:T(8,128)} %constant_dynamic-update-slice_fusion.16), kind=kOutput, calls=%fused_computation.1 | convolution fusion | flops 4873519104 | bytes 45613056 | tf_op jit(solution)/shard_map/dot_general | solution.py:203
  202.2 8.7 %fusion.106 = f32[1024,768]{0,1:T(8,128)S(1)} fusion(bf16[1024,3072]{1,0:T(8,128)(2,1)} %get-tuple-element.72, bf16[768,3072]{1,0:T(8,128)(2,1)} %param.23), kind=kOutput, calls=%fused_computation.211 | convolution fusion | flops 4831838208 | bytes 14155776 | tf_op jit(solution)/shard_map/dot_general | solution.py:203
  211.0 8.4 %fusion.11 = (f32[768]{0:T(1024)}, f32[1024]{0:T(1024)S(1)}, f32[1024,768]{0,1:T(8,128)S(1)}) fusion(bf16[1024,768]{0,1:T(8,128)(2,1)S(1)} %get-tuple-element.101, f32[1024]{0:T(1024)S(1)} %add_rsqrt_fusion, f32[768]{0:T(1024)S(1)} %convert_element_type.100, f32[1024,768]{0,1:T(8,128)S(1)} %fusion.106, bf16[1024,3072]{1,0:T(8,128)(2,1)S(1)} %copy-done.45, ...), kind=kOutput, calls=%fused_computation.23 | convolution fusion | flops 4838127616 | bytes 18888704 | tf_op jit(solution)/shard_map/dot_general | solution.py:203
  219.4 4.4 fusion.100
  223.8 1.9 convolution_convert_fusion.4.do_ref
  225.7 1.7 fusion.105
  228.4 27.9 %attn_bwd.5 = (bf16[2048,128]{1,0:T(8,128)(2,1)}, bf16[2048,128]{1,0:T(8,128)(2,1)}, bf16[2048,128]{1,0:T(8,128)(2,1)}, bf16[2048,128]{1,0:T(8,128)(2,1)}, f32[2,64,1024]{2,1,0:T(8,128)}) custom-call(s32[2]{0:T(128)} %copy-done.5, bf16[384,1024]{1,0:T(8,128)(2,1)} %copy-done.4, bf16[1024,384]{1,0:T(8,128)(2,1)} %fusion.24.q_ref, ...), custom_call_target="tpu_custom_call" | custom-call | flops 10737418240 | bytes 16777216 | tf_op jit(solution)/shard_map/attn_bwd/pallas_call | solution.py:183
  256.3 28.3 %attn_bwd.4 = (bf16[2048,128]{1,0:T(8,128)(2,1)}, bf16[2048,128]{1,0:T(8,128)(2,1)}, bf16[2048,128]{1,0:T(8,128)(2,1)}, bf16[2048,128]{1,0:T(8,128)(2,1)}, f32[2,64,1024]{2,1,0:T(8,128)}) custom-call(s32[2]{0:T(128)} %copy-done.5, bf16[384,1024]{1,0:T(8,128)(2,1)} %copy-done.4, bf16[1024,384]{1,0:T(8,128)(2,1)} %fusion.24.q_ref, ...), custom_call_target="tpu_custom_call" | custom-call | flops 10737418240 | bytes 16777216 | tf_op jit(solution)/shard_map/attn_bwd/pallas_call | solution.py:183
  284.6 27.9 %attn_bwd.3 = (bf16[2048,128]{1,0:T(8,128)(2,1)}, bf16[2048,128]{1,0:T(8,128)(2,1)}, bf16[2048,128]{1,0:T(8,128)(2,1)}, bf16[2048,128]{1,0:T(8,128)(2,1)}, f32[2,64,1024]{2,1,0:T(8,128)}) custom-call(s32[2]{0:T(128)} %copy-done.5, bf16[384,1024]{1,0:T(8,128)(2,1)} %copy-done.4, bf16[1024,384]{1,0:T(8,128)(2,1)} %fusion.24.q_ref, ...), custom_call_target="tpu_custom_call" | custom-call | flops 10737418240 | bytes 16777216 | tf_op jit(solution)/shard_map/attn_bwd/pallas_call | solution.py:183
  312.5 10.4 %fusion.89 = f32[768,3072]{1,0:T(8,128)} fusion(bf16[1024,3072]{1,0:T(8,128)(2,1)} %get-tuple-element.71, bf16[1024,768]{0,1:T(8,128)(2,1)S(1)} %get-tuple-element.101, f32[768]{0:T(1024)S(1)} %convert_element_type.100, f32[1024]{0:T(1024)S(1)} %add_rsqrt_fusion), kind=kOutput, calls=%fused_computation.202 | convolution fusion | flops 4834983936 | bytes 17308672 | tf_op jit(solution)/shard_map/dot_general | solution.py:203
  323.0 10.7 %fusion.91 = f32[768,3072]{1,0:T(8,128)} fusion(bf16[1024,3072]{1,0:T(8,128)(2,1)} %get-tuple-element.72, bf16[1024,768]{0,1:T(8,128)(2,1)S(1)} %get-tuple-element.101, f32[768]{0:T(1024)S(1)} %convert_element_type.100, f32[1024]{0:T(1024)S(1)} %add_rsqrt_fusion), kind=kOutput, calls=%fused_computation.203 | convolution fusion | flops 4834983936 | bytes 17308672 | tf_op jit(solution)/shard_map/dot_general | solution.py:203
  335.1 3.1 fusion.25
  338.2 1.5 collective-permute-start.20
  339.9 1.4 collective-permute-start.11
  342.7 3.0 fusion.27
  348.1 3.9 fusion.107
  352.0 3.0 fusion.26
  356.9 1.5 collective-permute-start.19
  358.4 1.6 pad_maximum_fusion.3
  360.0 14.8 %collective-permute-done.12 = f32[2,64,1024]{2,1,0:T(8,128)S(1)} collective-permute-done((f32[2,64,1024]{2,1,0:T(8,128)S(1)}, f32[2,64,1024]{2,1,0:T(8,128)S(1)}, u32[]{:S(2)}, u32[]{:S(2)}) %collective-permute-start.12) | collective-permute-done | bytes 524320 | tf_op jit(solution)/shard_map/ppermute | solution.py:221
  374.8 2.5 collective-permute-start.17
  377.4 8.7 %collective-permute-done.11 = f32[2,64,1024]{2,1,0:T(8,128)S(1)} collective-permute-done((f32[2,64,1024]{2,1,0:T(8,128)S(1)}, f32[2,64,1024]{2,1,0:T(8,128)S(1)}, u32[]{:S(2)}, u32[]{:S(2)}) %collective-permute-start.11) | collective-permute-done | bytes 524320 | tf_op jit(solution)/shard_map/ppermute | solution.py:221
  386.1 2.5 collective-permute-start.15
  390.2 12.7 %collective-permute-done.18 = f32[768,256]{0,1:T(8,128)S(1)} collective-permute-done((f32[768,256]{0,1:T(8,128)S(1)}, f32[768,256]{0,1:T(8,128)S(1)}, u32[]{:S(2)}, u32[]{:S(2)}) %collective-permute-start.18) | collective-permute-done | bytes 786464 | tf_op jit(solution)/shard_map/ppermute | solution.py:221
  402.9 2.5 collective-permute-start.14
  405.5 14.2 %collective-permute-done.19 = f32[768,256]{0,1:T(8,128)S(1)} collective-permute-done((f32[768,256]{0,1:T(8,128)S(1)}, f32[768,256]{0,1:T(8,128)S(1)}, u32[]{:S(2)}, u32[]{:S(2)}) %collective-permute-start.19) | collective-permute-done | bytes 786464 | tf_op jit(solution)/shard_map/ppermute | solution.py:221
  420.1 1.6 pad_maximum_fusion.2
  421.7 1.5 collective-permute-start.21
  423.2 5.9 %convolution_add_fusion = f32[2048,768]{1,0:T(8,128)} fusion(f32[2048,768]{1,0:T(8,128)S(1)} %fusion.107, bf16[768,768]{0,1:T(8,128)(2,1)} %get-tuple-element.82, bf16[2048,256]{1,0:T(8,128)(2,1)S(1)} %collective-permute-done.17, bf16[2048,256]{1,0:T(8,128)(2,1)S(1)} %collective-permute-done.16, bf16[2048,256]{1,0:T(8,128)(2,1)S(1)} %collective-permute-done.15), kind=kOutput, calls=%fused_computation.17 | convolution fusion | flops 2426929152 | bytes 16908288 | tf_op jit(solution)/shard_map/dot_general | solution.py:203
  429.1 4.0 multiply_reduce_fusion
  433.2 2.3 dynamic-slice_add_fusion
  435.5 2.3 copy.60
  437.7 2.6 fusion.87
  440.3 2.3 broadcast_select_fusion.5
  442.7 1.6 pad_maximum_fusion.1
  444.2 2.0 broadcast_select_fusion
  446.3 2.5 pad_maximum_fusion
  (200 shorter events, 30.5 us)
Async XLA Ops:
  0.6 37.5 %copy-start = (bf16[768,12,64]{0,2,1:T(8,128)(2,1)S(1)}, bf16[768,12,64]{0,2,1:T(8,128)(2,1)}, u32[]{:S(2)}) copy-start(bf16[768,12,64]{0,2,1:T(8,128)(2,1)} %param.18) | copy-start | bytes 3538948
  0.7 11.3 %copy-start.16 = (bf16[768,12,64]{0,2,1:T(8,128)(2,1)S(1)}, bf16[768,12,64]{0,2,1:T(8,128)(2,1)}, u32[]{:S(2)}) copy-start(bf16[768,12,64]{0,2,1:T(8,128)(2,1)} %param.19) | copy-start | bytes 3538948
  0.7 42.7 %collective-permute-start.6 = (bf16[2048,768]{1,0:T(8,128)(2,1)}, bf16[2048,768]{1,0:T(8,128)(2,1)}, u32[]{:S(2)}, u32[]{:S(2)}) collective-permute-start(bf16[2048,768]{1,0:T(8,128)(2,1)} %param.14), channel_id=1, source_target_pairs={{0,1},{1,0},{2,3},{3,2},{4,5},{5,4},{6,7},{7,6}} | collective-permute-start | bytes 9437192 | tf_op jit(solution)/shard_map/ppermute | solution.py:218
  2.5 30.6 %collective-permute-start.4 = (bf16[256,768]{0,1:T(8,128)(2,1)S(1)}, bf16[256,768]{0,1:T(8,128)(2,1)S(1)}, u32[]{:S(2)}, u32[]{:S(2)}) collective-permute-start(bf16[256,768]{0,1:T(8,128)(2,1)S(1)} %copy.27), channel_id=1, source_target_pairs={{0,1},{1,0},{2,3},{3,2},{4,5},{5,4},{6,7},{7,6}} | collective-permute-start | bytes 1179656 | tf_op jit(solution)/shard_map/ppermute | solution.py:218
  2.7 18.5 %collective-permute-start.3 = (bf16[256,768]{0,1:T(8,128)(2,1)S(1)}, bf16[256,768]{0,1:T(8,128)(2,1)}, u32[]{:S(2)}, u32[]{:S(2)}) collective-permute-start(bf16[256,768]{0,1:T(8,128)(2,1)S(1)} %copy.27), channel_id=1, source_target_pairs={{0,2},{1,3},{2,0},{3,1},{4,6},{5,7},{6,4},{7,5}} | collective-permute-start | bytes 1179656 | tf_op jit(solution)/shard_map/ppermute | solution.py:221
  6.2 133.5 %collective-permute-start.1 = (f32[256,768]{0,1:T(8,128)}, f32[256,768]{0,1:T(8,128)}, u32[]{:S(2)}, u32[]{:S(2)}) collective-permute-start(f32[256,768]{0,1:T(8,128)} %copy.24), channel_id=1, source_target_pairs={{0,1},{1,0},{2,3},{3,2},{4,5},{5,4},{6,7},{7,6}} | collective-permute-start | bytes 2359304 | tf_op jit(solution)/shard_map/ppermute | solution.py:218
  6.8 36.3 %collective-permute-start = (f32[256,768]{0,1:T(8,128)}, f32[256,768]{0,1:T(8,128)}, u32[]{:S(2)}, u32[]{:S(2)}) collective-permute-start(f32[256,768]{0,1:T(8,128)} %copy.24), channel_id=1, source_target_pairs={{0,2},{1,3},{2,0},{3,1},{4,6},{5,7},{6,4},{7,5}} | collective-permute-start | bytes 2359304 | tf_op jit(solution)/shard_map/ppermute | solution.py:221
  7.1 4.1 copy-start.17
  7.1 7.2 %copy-start.43 = (bf16[2048,768]{1,0:T(8,128)(2,1)S(1)}, bf16[2048,768]{1,0:T(8,128)(2,1)}, u32[]{:S(2)}) copy-start(bf16[2048,768]{1,0:T(8,128)(2,1)} %param.14) | copy-start | bytes 9437188
  16.8 4.8 %copy-start.41 = (bf16[768]{0:T(1024)(128)(2,1)S(1)}, bf16[768]{0:T(1024)(128)(2,1)}, u32[]{:S(2)}) copy-start(bf16[768]{0:T(1024)(128)(2,1)} %param.22) | copy-start | bytes 4612
  16.8 4.8 %copy-start.42 = (bf16[768]{0:T(1024)(128)(2,1)S(1)}, bf16[768]{0:T(1024)(128)(2,1)}, u32[]{:S(2)}) copy-start(bf16[768]{0:T(1024)(128)(2,1)} %param.17) | copy-start | bytes 4612
  21.3 12.7 %collective-permute-start.5 = (bf16[256,768]{0,1:T(8,128)(2,1)}, bf16[256,768]{0,1:T(8,128)(2,1)}, u32[]{:S(2)}, u32[]{:S(2)}) collective-permute-start(bf16[256,768]{0,1:T(8,128)(2,1)} %collective-permute-done.3), channel_id=1, source_target_pairs={{0,1},{1,0},{2,3},{3,2},{4,5},{5,4},{6,7},{7,6}} | collective-permute-start | bytes 1179656 | tf_op jit(solution)/shard_map/ppermute | solution.py:218
  21.7 79.8 %copy-start.5 = (s32[2]{0:T(128)}, s32[2]{0:T(128)S(1)}, u32[]{:S(2)}) copy-start(s32[2]{0:T(128)S(1)} %pad_add_fusion.len_ref) | copy-start | bytes 28
  21.7 16.5 %copy-start.38 = (f32[768]{0:T(1024)}, f32[768]{0:T(1024)S(1)}, u32[]{:S(2)}) copy-start(f32[768]{0:T(1024)S(1)} %convert_element_type.86) | copy-start | bytes 9220
  24.1 77.4 %copy-start.1 = (bf16[2048,384]{1,0:T(8,128)(2,1)}, bf16[2048,384]{1,0:T(8,128)(2,1)S(1)}, u32[]{:S(2)}) copy-start(bf16[2048,384]{1,0:T(8,128)(2,1)S(1)} %copy.33.k0_ref) | copy-start | bytes 4718596
  37.5 4.2 copy-start.36
  43.1 58.3 %copy-start.4 = (bf16[384,1024]{1,0:T(8,128)(2,1)}, bf16[384,1024]{1,0:T(8,128)(2,1)S(1)}, u32[]{:S(2)}) copy-start(bf16[384,1024]{1,0:T(8,128)(2,1)S(1)} %copy.32.qt_ref) | copy-start | bytes 2359300
  43.2 98.7 %collective-permute-start.2 = (f32[256,768]{0,1:T(8,128)}, f32[256,768]{0,1:T(8,128)}, u32[]{:S(2)}, u32[]{:S(2)}) collective-permute-start(f32[256,768]{0,1:T(8,128)} %collective-permute-done), channel_id=1, source_target_pairs={{0,1},{1,0},{2,3},{3,2},{4,5},{5,4},{6,7},{7,6}} | collective-permute-start | bytes 2359304 | tf_op jit(solution)/shard_map/ppermute | solution.py:218
  81.1 40.5 %collective-permute-start.7 = (f32[2,72,1024]{2,1,0:T(8,128)S(1)}, f32[2,72,1024]{2,1,0:T(8,128)S(1)}, u32[]{:S(2)}, u32[]{:S(2)}) collective-permute-start(f32[2,72,1024]{2,1,0:T(8,128)S(1)} %attn_fwd.3), channel_id=1, source_target_pairs={{0,2},{1,3},{2,0},{3,1},{4,6},{5,7},{6,4},{7,5}} | collective-permute-start | bytes 1769480 | tf_op jit(solution)/shard_map/ppermute | solution.py:221
  101.4 20.3 %collective-permute-start.8 = (f32[2,72,1024]{2,1,0:T(8,128)S(1)}, f32[2,72,1024]{2,1,0:T(8,128)S(1)}, u32[]{:S(2)}, u32[]{:S(2)}) collective-permute-start(f32[2,72,1024]{2,1,0:T(8,128)S(1)} %attn_fwd.4), channel_id=1, source_target_pairs={{0,2},{1,3},{2,0},{3,1},{4,6},{5,7},{6,4},{7,5}} | collective-permute-start | bytes 1769480 | tf_op jit(solution)/shard_map/ppermute | solution.py:221
  121.6 14.6 %collective-permute-start.9 = (f32[2,72,1024]{2,1,0:T(8,128)S(1)}, f32[2,72,1024]{2,1,0:T(8,128)S(1)}, u32[]{:S(2)}, u32[]{:S(2)}) collective-permute-start(f32[2,72,1024]{2,1,0:T(8,128)S(1)} %attn_fwd.5), channel_id=1, source_target_pairs={{0,2},{1,3},{2,0},{3,1},{4,6},{5,7},{6,4},{7,5}} | collective-permute-start | bytes 1769480 | tf_op jit(solution)/shard_map/ppermute | solution.py:221
  122.0 19.8 %copy-start.10 = (f32[2,64,1024]{2,1,0:T(8,128)}, f32[2,64,1024]{2,1,0:T(8,128)S(1)}, u32[]{:S(2)}) copy-start(f32[2,64,1024]{2,1,0:T(8,128)S(1)} %fusion.53) | copy-start | bytes 1572868
  136.4 7.5 %copy-start.12 = (f32[2,64,1024]{2,1,0:T(8,128)}, f32[2,64,1024]{2,1,0:T(8,128)S(1)}, u32[]{:S(2)}) copy-start(f32[2,64,1024]{2,1,0:T(8,128)S(1)} %fusion.51) | copy-start | bytes 1572868
  136.4 8.1 %copy-start.14 = (bf16[12,64,768]{2,1,0:T(8,128)(2,1)S(1)}, bf16[12,64,768]{2,1,0:T(8,128)(2,1)}, u32[]{:S(2)}) copy-start(bf16[12,64,768]{2,1,0:T(8,128)(2,1)} %param.21) | copy-start | bytes 3538948
  136.5 9.1 %copy-start.6 = (bf16[6,64,1024]{2,1,0:T(8,128)(2,1)}, bf16[6,64,1024]{2,1,0:T(8,128)(2,1)S(1)}, u32[]{:S(2)}) copy-start(bf16[6,64,1024]{2,1,0:T(8,128)(2,1)S(1)} %fusion.28) | copy-start | bytes 2359300
  136.5 9.1 %collective-permute-start.10 = (bf16[384,1024]{1,0:T(8,128)(2,1)S(1)}, bf16[384,1024]{1,0:T(8,128)(2,1)S(1)}, u32[]{:S(2)}, u32[]{:S(2)}) collective-permute-start(bf16[384,1024]{1,0:T(8,128)(2,1)S(1)} %bitcast.92), channel_id=1, source_target_pairs={{0,1},{1,0},{2,3},{3,2},{4,5},{5,4},{6,7},{7,6}} | collective-permute-start | bytes 2359304 | tf_op jit(solution)/shard_map/ppermute | solution.py:218
  144.5 4.3 slice-start
  145.6 3.2 slice-start.1
  145.6 3.2 copy-start.18
  145.6 11.8 %slice-start.2 = ((s8[4718592]{0:T(1024)(128)(4,1)}), s8[524288]{0:T(1024)(128)(4,1)S(1)}, s32[]{:S(2)}) async-start(s8[4718592]{0:T(1024)(128)(4,1)} %bitcast.101), calls=%async_computation.2 | async-start | bytes 1048576
  148.8 8.5 %slice-start.3 = ((s8[4718592]{0:T(1024)(128)(4,1)}), s8[4194304]{0:T(1024)(128)(4,1)S(1)}, s32[]{:S(2)}) async-start(s8[4718592]{0:T(1024)(128)(4,1)} %bitcast.101), calls=%async_computation.3 | async-start | bytes 8388608
  202.2 8.7 %copy-start.45 = (bf16[1024,3072]{1,0:T(8,128)(2,1)S(1)}, bf16[1024,3072]{1,0:T(8,128)(2,1)}, u32[]{:S(2)}) copy-start(bf16[1024,3072]{1,0:T(8,128)(2,1)} %get-tuple-element.71) | copy-start | bytes 18874372
  219.4 4.4 copy-start.15
  322.9 10.8 %copy-start.35 = (bf16[2048,128]{1,0:T(8,128)(2,1)S(1)}, bf16[2048,128]{1,0:T(8,128)(2,1)}, u32[]{:S(2)}) copy-start(bf16[2048,128]{1,0:T(8,128)(2,1)} %get-tuple-element.39) | copy-start | bytes 1572868
  322.9 10.9 %copy-start.23 = (f32[2,64,1024]{2,1,0:T(8,128)S(1)}, f32[2,64,1024]{2,1,0:T(8,128)}, u32[]{:S(2)}) copy-start(f32[2,64,1024]{2,1,0:T(8,128)} %get-tuple-element.28) | copy-start | bytes 1572868
  322.9 10.9 %copy-start.34 = (bf16[2048,128]{1,0:T(8,128)(2,1)S(1)}, bf16[2048,128]{1,0:T(8,128)(2,1)}, u32[]{:S(2)}) copy-start(bf16[2048,128]{1,0:T(8,128)(2,1)} %get-tuple-element.40) | copy-start | bytes 1572868
  322.9 11.1 %copy-start.24 = (bf16[2048,128]{1,0:T(8,128)(2,1)S(1)}, bf16[2048,128]{1,0:T(8,128)(2,1)}, u32[]{:S(2)}) copy-start(bf16[2048,128]{1,0:T(8,128)(2,1)} %get-tuple-element.34) | copy-start | bytes 1572868
  322.9 11.1 %copy-start.25 = (bf16[2048,128]{1,0:T(8,128)(2,1)S(1)}, bf16[2048,128]{1,0:T(8,128)(2,1)}, u32[]{:S(2)}) copy-start(bf16[2048,128]{1,0:T(8,128)(2,1)} %get-tuple-element.33) | copy-start | bytes 1572868
  323.0 11.1 %copy-start.44 = (bf16[2048,768]{1,0:T(8,128)(2,1)S(1)}, bf16[2048,768]{1,0:T(8,128)(2,1)}, u32[]{:S(2)}) copy-start(bf16[2048,768]{1,0:T(8,128)(2,1)} %param.14) | copy-start | bytes 9437188
  333.8 23.1 %collective-permute-start.13 = (f32[2,64,1024]{2,1,0:T(8,128)S(1)}, f32[2,64,1024]{2,1,0:T(8,128)S(1)}, u32[]{:S(2)}, u32[]{:S(2)}) collective-permute-start(f32[2,64,1024]{2,1,0:T(8,128)S(1)} %copy-done.23), channel_id=1, source_target_pairs={{0,2},{1,3},{2,0},{3,1},{4,6},{5,7},{6,4},{7,5}} | collective-permute-start | bytes 1572872 | tf_op jit(solution)/shard_map/ppermute | solution.py:221
  335.1 4.6 %copy-start.32 = (bf16[2048,128]{1,0:T(8,128)(2,1)S(1)}, bf16[2048,128]{1,0:T(8,128)(2,1)}, u32[]{:S(2)}) copy-start(bf16[2048,128]{1,0:T(8,128)(2,1)} %get-tuple-element.37) | copy-start | bytes 1572868
  335.1 4.7 %copy-start.33 = (bf16[2048,128]{1,0:T(8,128)(2,1)S(1)}, bf16[2048,128]{1,0:T(8,128)(2,1)}, u32[]{:S(2)}) copy-start(bf16[2048,128]{1,0:T(8,128)(2,1)} %get-tuple-element.35) | copy-start | bytes 1572868
  335.1 4.8 %copy-start.22 = (f32[2,64,1024]{2,1,0:T(8,128)S(1)}, f32[2,64,1024]{2,1,0:T(8,128)}, u32[]{:S(2)}) copy-start(f32[2,64,1024]{2,1,0:T(8,128)} %get-tuple-element.27) | copy-start | bytes 1572868
  335.1 4.8 %copy-start.21 = (f32[2,64,1024]{2,1,0:T(8,128)S(1)}, f32[2,64,1024]{2,1,0:T(8,128)}, u32[]{:S(2)}) copy-start(f32[2,64,1024]{2,1,0:T(8,128)} %get-tuple-element.26) | copy-start | bytes 1572868
  335.1 6.3 %copy-start.31 = (bf16[2048,128]{1,0:T(8,128)(2,1)S(1)}, bf16[2048,128]{1,0:T(8,128)(2,1)}, u32[]{:S(2)}) copy-start(bf16[2048,128]{1,0:T(8,128)(2,1)} %get-tuple-element.29) | copy-start | bytes 1572868
  335.1 6.3 %copy-start.29 = (bf16[2048,128]{1,0:T(8,128)(2,1)S(1)}, bf16[2048,128]{1,0:T(8,128)(2,1)}, u32[]{:S(2)}) copy-start(bf16[2048,128]{1,0:T(8,128)(2,1)} %get-tuple-element.30) | copy-start | bytes 1572868
  338.2 51.6 %collective-permute-start.20 = (f32[768,256]{0,1:T(8,128)S(1)}, f32[768,256]{0,1:T(8,128)S(1)}, u32[]{:S(2)}, u32[]{:S(2)}) collective-permute-start(f32[768,256]{0,1:T(8,128)S(1)} %fusion.25), channel_id=1, source_target_pairs={{0,2},{1,3},{2,0},{3,1},{4,6},{5,7},{6,4},{7,5}} | collective-permute-start | bytes 2359304 | tf_op jit(solution)/shard_map/ppermute | solution.py:221
  339.9 35.0 %collective-permute-start.12 = (f32[2,64,1024]{2,1,0:T(8,128)S(1)}, f32[2,64,1024]{2,1,0:T(8,128)S(1)}, u32[]{:S(2)}, u32[]{:S(2)}) collective-permute-start(f32[2,64,1024]{2,1,0:T(8,128)S(1)} %copy-done.22), channel_id=1, source_target_pairs={{0,2},{1,3},{2,0},{3,1},{4,6},{5,7},{6,4},{7,5}} | collective-permute-start | bytes 1572872 | tf_op jit(solution)/shard_map/ppermute | solution.py:221
  339.9 46.1 %collective-permute-start.11 = (f32[2,64,1024]{2,1,0:T(8,128)S(1)}, f32[2,64,1024]{2,1,0:T(8,128)S(1)}, u32[]{:S(2)}, u32[]{:S(2)}) collective-permute-start(f32[2,64,1024]{2,1,0:T(8,128)S(1)} %copy-done.21), channel_id=1, source_target_pairs={{0,2},{1,3},{2,0},{3,1},{4,6},{5,7},{6,4},{7,5}} | collective-permute-start | bytes 1572872 | tf_op jit(solution)/shard_map/ppermute | solution.py:221
  342.6 3.2 copy-start.27
  342.6 3.2 copy-start.28
  345.7 57.3 %collective-permute-start.18 = (f32[768,256]{0,1:T(8,128)S(1)}, f32[768,256]{0,1:T(8,128)S(1)}, u32[]{:S(2)}, u32[]{:S(2)}) collective-permute-start(f32[768,256]{0,1:T(8,128)S(1)} %fusion.27), channel_id=1, source_target_pairs={{0,2},{1,3},{2,0},{3,1},{4,6},{5,7},{6,4},{7,5}} | collective-permute-start | bytes 2359304 | tf_op jit(solution)/shard_map/ppermute | solution.py:221
  352.0 3.0 copy-start.19
  356.9 62.8 %collective-permute-start.19 = (f32[768,256]{0,1:T(8,128)S(1)}, f32[768,256]{0,1:T(8,128)S(1)}, u32[]{:S(2)}, u32[]{:S(2)}) collective-permute-start(f32[768,256]{0,1:T(8,128)S(1)} %fusion.26), channel_id=1, source_target_pairs={{0,2},{1,3},{2,0},{3,1},{4,6},{5,7},{6,4},{7,5}} | collective-permute-start | bytes 2359304 | tf_op jit(solution)/shard_map/ppermute | solution.py:221
  374.8 48.3 %collective-permute-start.17 = (bf16[2048,256]{1,0:T(8,128)(2,1)S(1)}, bf16[2048,256]{1,0:T(8,128)(2,1)S(1)}, u32[]{:S(2)}, u32[]{:S(2)}) collective-permute-start(bf16[2048,256]{1,0:T(8,128)(2,1)S(1)} %constant_dynamic-update-slice_fusion.10), channel_id=1, source_target_pairs={{0,1},{1,0},{2,3},{3,2},{4,5},{5,4},{6,7},{7,6}} | collective-permute-start | bytes 3145736 | tf_op jit(solution)/shard_map/ppermute | solution.py:218
  386.1 37.1 %collective-permute-start.15 = (bf16[2048,256]{1,0:T(8,128)(2,1)S(1)}, bf16[2048,256]{1,0:T(8,128)(2,1)S(1)}, u32[]{:S(2)}, u32[]{:S(2)}) collective-permute-start(bf16[2048,256]{1,0:T(8,128)(2,1)S(1)} %constant_dynamic-update-slice_fusion.6), channel_id=1, source_target_pairs={{0,1},{1,0},{2,3},{3,2},{4,5},{5,4},{6,7},{7,6}} | collective-permute-start | bytes 3145736 | tf_op jit(solution)/shard_map/ppermute | solution.py:218
  388.8 14.2 %copy-start.8 = (bf16[6,64,1024]{2,1,0:T(8,128)(2,1)}, bf16[6,64,1024]{2,1,0:T(8,128)(2,1)S(1)}, u32[]{:S(2)}) copy-start(bf16[6,64,1024]{2,1,0:T(8,128)(2,1)S(1)} %fusion.23) | copy-start | bytes 2359300
  389.8 33.3 %collective-permute-start.16 = (bf16[2048,256]{1,0:T(8,128)(2,1)S(1)}, bf16[2048,256]{1,0:T(8,128)(2,1)S(1)}, u32[]{:S(2)}, u32[]{:S(2)}) collective-permute-start(bf16[2048,256]{1,0:T(8,128)(2,1)S(1)} %constant_dynamic-update-slice_fusion.8), channel_id=1, source_target_pairs={{0,1},{1,0},{2,3},{3,2},{4,5},{5,4},{6,7},{7,6}} | collective-permute-start | bytes 3145736 | tf_op jit(solution)/shard_map/ppermute | solution.py:218
  402.9 26.1 %collective-permute-start.14 = (bf16[384,1024]{1,0:T(8,128)(2,1)S(1)}, bf16[384,1024]{1,0:T(8,128)(2,1)S(1)}, u32[]{:S(2)}, u32[]{:S(2)}) collective-permute-start(bf16[384,1024]{1,0:T(8,128)(2,1)S(1)} %bitcast.97), channel_id=1, source_target_pairs={{0,1},{1,0},{2,3},{3,2},{4,5},{5,4},{6,7},{7,6}} | collective-permute-start | bytes 2359304 | tf_op jit(solution)/shard_map/ppermute | solution.py:218
  421.7 22.5 %collective-permute-start.21 = (f32[2,768,384]{1,2,0:T(8,128)}, f32[2,768,384]{1,2,0:T(8,128)}, u32[]{:S(2)}, u32[]{:S(2)}) collective-permute-start(f32[2,768,384]{1,2,0:T(8,128)} %pad_maximum_fusion.2), channel_id=1, source_target_pairs={{0,1},{1,0},{2,3},{3,2},{4,5},{5,4},{6,7},{7,6}} | collective-permute-start | bytes 7077896 | tf_op jit(solution)/shard_map/ppermute | solution.py:218
  423.2 5.9 %copy-start.37 = (f32[1024]{0:T(1024)S(1)}, f32[1024]{0:T(1024)}, u32[]{:S(2)}) copy-start(f32[1024]{0:T(1024)} %copy-done.36) | copy-start | bytes 12292
  423.2 5.9 %copy-start.39 = (f32[768]{0:T(1024)S(1)}, f32[768]{0:T(1024)}, u32[]{:S(2)}) copy-start(f32[768]{0:T(1024)} %copy-done.38) | copy-start | bytes 9220
  429.0 4.1 copy-start.40
  429.1 4.0 copy-start.20
  (8 other events, 12.0 us)
